TPU v7x, 32 devices: a whole 2x2x4 slice. The times are simulated.
32 devices in a mesh: rep: 4 (over x, y), dp: 8 (over z, core).
Axes of the slice: x: 2, y: 2, z: 4, core: 2. Of those that a mesh axis runs over, the one named last changes fastest.
Arguments:
- a: bfloat16 [32, 4, 8192, 896], P(('rep', 'dp')), parts along dimension 0
- g: bfloat16 [32, 4, 8192, 2560], P(('rep', 'dp')), parts along dimension 0
Outputs:
- output: bfloat16 [16, 896, 2560], P('rep'), parts along dimension 0
There are 4 independent parts. A program takes and returns all parts, laid end to end along the dimension named above; each array names one.
All inputs are finite; a program needn't handle non-finite values.
Results may differ from a plain program's by a relative error of at most 0.012.
Values are sent between devices in bfloat16 or wider.
A program may use at most 2 GiB of HBM per device.

v0:
```python
import jax
import jax.numpy as jnp


def solution(mesh):
    groups = mesh.shape["rep"]

    def step(a, g):
        a, g = (t.reshape(groups, -1, *t.shape[1:]) for t in (a, g))
        sums = jnp.einsum("rsntd,rsntf->rndf", a, g, preferred_element_type=jnp.float32)
        return sums.astype(jnp.bfloat16).reshape(-1, *sums.shape[2:])

    return step
```

profile of v0, /device:TPU:0, one launch (start us, length us, event | category | flops | bytes accessed | tf_op | source)
XLA Modules:
  0.0 879.1 jit_solution(4046563080630735973)
XLA Ops:
  0.0 166.8 %fusion.3 = f32[1,4,896,2560]{3,2,1,0:T(8,128)} fusion(bf16[1,4,8192,2560]{3,2,1,0:T(8,128)(2,1)} %param.1, bf16[1,4,8192,896]{3,2,1,0:T(8,128)(2,1)} %param), kind=kOutput, calls=%fused_computation.3 | convolution fusion | flops 150323855360 | bytes 263192576 | tf_op jit(solution)/rsntd,rsntf->rndf/dot_general | solution.py:10
  166.8 712.3 %all-reduce.2 = bf16[1,4,896,2560]{3,2,1,0:T(8,128)(2,1)} all-reduce(f32[1,4,896,2560]{3,2,1,0:T(8,128)} %fusion.3), channel_id=1, replica_groups=[4,8]<=[32], use_global_device_ids=true, to_apply=%add.clone | all-reduce | flops 9175040 | bytes 55050240 | tf_op jit(solution)/rsntd,rsntf->rndf/dot_general | solution.py:10
where the time goes:
time: 879 us
  blocking collectives  712 us (81%)
  matrix products  167 us (19%)
    dot_general x1, blocking collectives, step(): jnp.einsum('rsntd,rsntf->rndf', a, g, preferred_element_type=jnp.float32)  712 us
    dot_general x1, matrix products, step(): jnp.einsum('rsntd,rsntf->rndf', a, g, preferred_element_type=jnp.float32)  167 us

commit v1 on v0

v1 whole, which is shorter than its diff:
```python
import functools

import jax
import jax.numpy as jnp
from jax import lax
from jax.experimental import pallas as pl
from jax.experimental.pallas import tpu as pltpu

COMBINE_LAG = {0: 1, 1: 6, 2: 3, 3: 1}
DELIVER_LAG = {0: 8, 1: 6, 2: 8, 3: 11}
KEEP = {0: 1, 1: 4, 2: 4, 3: 1}
OWN, PAIR_OUT, PAIR_IN, FROM_A, FROM_B, PART, RES = 7, 2, 12, 12, 8, 4, 14
SLICES = 8
PIECES = 2


def kernel(width, a_hbm, g_hbm, out_hbm, a_buf, g_buf, own, pair_out, pair_in, from_a, from_b, part, res,
           a_sem, g_sem, pair_ssem, pair_rsem, a_rsem, b_rsem, part_ssem, res_rsem, left_ssem, right_ssem,
           swap_ssem, store_sem, out_rsem):
    matrices, tokens, rows = a_hbm.shape
    per = g_hbm.shape[2] // width
    chunks = matrices * per
    half = rows // 2
    piece = half // PIECES
    depth = tokens // SLICES

    me = lax.axis_index("dp")
    chip, core = me // 2, me % 2
    place = chip + core * (3 - 2 * chip)
    step_to = 2 - 4 * core
    partner = me + 1 - 2 * core
    up, down = me + step_to, me - step_to

    barrier = pltpu.get_barrier_semaphore()

    def hello(device):
        pl.semaphore_signal(barrier, inc=1, device_id={"dp": device}, device_id_type=pl.DeviceIdType.MESH)

    hello(partner)
    pl.when(place > 0)(lambda: hello(down))
    pl.when(place < 3)(lambda: hello(up))

    def a_load(n, k):
        return pltpu.make_async_copy(
            a_hbm.at[n, pl.ds(k * depth, depth), :], a_buf.at[n % 2, pl.ds(k * depth, depth), :], a_sem.at[n % 2, k])

    def g_load(j):
        return pltpu.make_async_copy(
            g_hbm.at[j // per, :, pl.ds(pl.multiple_of((j % per) * width, width), width)], g_buf.at[j % 2],
            g_sem.at[j % 2])

    for k in range(SLICES):
        a_load(0, k).start()
        if k == 0:
            g_load(0).start()
    pl.semaphore_wait(barrier, 1 + (place > 0).astype(jnp.int32) + (place < 3).astype(jnp.int32))

    def remote(src, dst, ssem, rsem, device):
        return pltpu.make_async_remote_copy(
            src_ref=src, dst_ref=dst, send_sem=ssem, recv_sem=rsem, device_id={"dp": device},
            device_id_type=pl.DeviceIdType.MESH)

    def strip(q):
        return pl.ds(q * piece, piece)

    def pair_copy(j):
        return remote(pair_out.at[j % PAIR_OUT], pair_in.at[j % PAIR_IN], pair_ssem.at[j % PAIR_OUT],
                      pair_rsem.at[j % PAIR_IN], partner)

    def part_copy(j, q, box, rsem, slots, device):
        return remote(part.at[j % PART, strip(q), :], box.at[j % slots, strip(q), :], part_ssem.at[j % PART, q],
                      rsem.at[j % slots, q], device)

    def res_copy(j, q, ssem, device):
        return remote(res.at[j % RES, strip(q), :], res.at[j % RES, strip(q), :], ssem.at[j % RES, q],
                      res_rsem.at[j % RES, q], device)

    def place_of(j, q):
        return out_hbm.at[j // per, pl.ds(pl.multiple_of(core * half + q * piece, 16), piece),
                          pl.ds(pl.multiple_of((j % per) * width, width), width)]

    def swap_copy(j, q):
        return remote(res.at[j % RES, strip(q), :], place_of(j, q), swap_ssem.at[j % RES, q], out_rsem.at[j // per],
                      partner)

    def store_copy(j, q):
        return pltpu.make_async_copy(res.at[j % RES, strip(q), :], place_of(j, q), store_sem.at[j % RES, q])

    def mine(j, q):
        return (own[j % OWN, pl.ds(pl.multiple_of(core * half + q * piece, 16), piece), :]
                + pair_in[j % PAIR_IN, strip(q), :].astype(jnp.float32))

    def outgoing(d, j, q):
        copies = [swap_copy(j, q), store_copy(j, q)]
        if d == 1:
            copies = [res_copy(j, q, right_ssem, up), res_copy(j, q, left_ssem, down)] + copies
        if d == 2:
            copies = [res_copy(j, q, right_ssem, up)] + copies
        return copies

    def finish(d, j):
        for q in range(PIECES):
            outs = outgoing(d, j, q)
            for c in outs[:-1]:
                c.wait_send()
            outs[-1].wait()

    def combine(d, j):
        pair_copy(j).wait_recv()
        for q in range(PIECES):
            total = mine(j, q)
            if d == 2:
                part_copy(j, q, from_a, a_rsem, FROM_A, up).wait_recv()
                total += from_a[j % FROM_A, strip(q), :].astype(jnp.float32)
            if d == 1:
                part_copy(j, q, from_a, a_rsem, FROM_A, down).wait_recv()
                total += from_a[j % FROM_A, strip(q), :].astype(jnp.float32)
                part_copy(j, q, from_b, b_rsem, FROM_B, up).wait_recv()
                total += from_b[j % FROM_B, strip(q), :].astype(jnp.float32)
            if d == 1:
                res[j % RES, strip(q), :] = total.astype(jnp.bfloat16)
                for c in outgoing(1, j, q):
                    c.start()
                continue
            if d == 2:
                copy = functools.partial(part_copy, q=q, box=from_b, rsem=b_rsem, slots=FROM_B, device=down)
            else:
                copy = functools.partial(part_copy, q=q, box=from_a, rsem=a_rsem, slots=FROM_A,
                                         device=up if d == 0 else down)
            pl.when(j >= PART)(lambda: copy(j - PART).wait_send())
            part[j % PART, strip(q), :] = total.astype(jnp.bfloat16)
            copy(j).start()

    def deliver(d, j):
        for q in range(PIECES):
            res_copy(j, q, right_ssem, up).wait_recv()
            for c in outgoing(d, j, q):
                c.start()

    def each_place(f):
        for d in range(4):
            pl.when(place == d)(functools.partial(f, d))

    def step(s, _):
        @pl.when(s < chunks)
        def _():
            n, t = s // per, s % per

            @pl.when(s + 1 < chunks)
            def _():
                g_load(s + 1).start()

            @pl.when((n + 1 < matrices) & (t < SLICES))
            def _():
                a_load(n + 1, t).start()

            @pl.when(t == 0)
            def _():
                for k in range(SLICES):
                    a_load(n, k).wait()

            g_load(s).wait()
            own[s % OWN] = lax.dot_general(
                a_buf[n % 2], g_buf[s % 2], (((0,), (0,)), ((), ())), preferred_element_type=jnp.float32)
            pl.when(s >= PAIR_OUT)(lambda: pair_copy(s - PAIR_OUT).wait_send())
            pair_out[s % PAIR_OUT] = own[
                s % OWN, pl.ds(pl.multiple_of((1 - core) * half, 16), half), :].astype(jnp.bfloat16)
            pair_copy(s).start()

        def stages(d):
            j = s - COMBINE_LAG[d]

            @pl.when((j >= 0) & (j < chunks))
            def _():
                if d == 1:
                    pl.when(j >= KEEP[d])(lambda: finish(d, j - KEEP[d]))
                combine(d, j)

            if d != 1:
                i = s - DELIVER_LAG[d]

                @pl.when((i >= 0) & (i < chunks))
                def _():
                    pl.when(i >= KEEP[d])(lambda: finish(d, i - KEEP[d]))
                    deliver(d, i)

        each_place(stages)
        return 0

    lax.fori_loop(0, chunks + max(DELIVER_LAG.values()), step, 0)

    for j in range(chunks - PAIR_OUT, chunks):
        pair_copy(j).wait_send()

    def flush(d):
        for j in range(chunks - KEEP[d], chunks):
            finish(d, j)
        if d != 1:
            for j in range(chunks - PART, chunks):
                for q in range(PIECES):
                    part_copy(j, q, from_a, a_rsem, FROM_A, down).wait_send()

    each_place(flush)
    for n in range(matrices):
        theirs = out_hbm.at[n, pl.ds(pl.multiple_of((1 - core) * half, 16), half), :]
        remote(theirs, theirs, out_rsem.at[n], out_rsem.at[n], partner).wait_recv()


def sums(a, g, width=256):
    a, g = a[0], g[0]
    matrices, tokens, rows = a.shape
    columns = g.shape[2]
    half = rows // 2
    bf16 = jnp.bfloat16
    dma = pltpu.SemaphoreType.DMA
    return pl.pallas_call(
        functools.partial(kernel, width),
        out_shape=jax.ShapeDtypeStruct((matrices, rows, columns), bf16),
        in_specs=[pl.BlockSpec(memory_space=pl.ANY)] * 2,
        out_specs=pl.BlockSpec(memory_space=pl.ANY),
        scratch_shapes=[
            pltpu.VMEM((2, tokens, rows), bf16),
            pltpu.VMEM((2, tokens, width), bf16),
            pltpu.VMEM((OWN, rows, width), jnp.float32),
            pltpu.VMEM((PAIR_OUT, half, width), bf16),
            pltpu.VMEM((PAIR_IN, half, width), bf16),
            pltpu.VMEM((FROM_A, half, width), bf16),
            pltpu.VMEM((FROM_B, half, width), bf16),
            pltpu.VMEM((PART, half, width), bf16),
            pltpu.VMEM((RES, half, width), bf16),
            dma((2, SLICES)),
            dma((2,)),
            dma((PAIR_OUT,)),
            dma((PAIR_IN,)),
            dma((FROM_A, PIECES)),
            dma((FROM_B, PIECES)),
            dma((PART, PIECES)),
            dma((RES, PIECES)),
            dma((RES, PIECES)),
            dma((RES, PIECES)),
            dma((RES, PIECES)),
            dma((RES, PIECES)),
            dma((matrices,)),
        ],
        compiler_params=pltpu.CompilerParams(collective_id=0, has_side_effects=True, vmem_limit_bytes=67043328),
        name="grad_sums",
    )(a, g)


def solution(mesh):
    P = jax.sharding.PartitionSpec
    return jax.shard_map(
        sums, mesh=mesh, in_specs=(P(("rep", "dp")), P(("rep", "dp"))), out_specs=P("rep"), check_vma=False)
```

time: 879 us -> 259 us (0.29)
  blocking collectives: 712 us -> 0 us
  Pallas kernels: 0 us -> 243 us
  matrix products: 167 us -> 0 us
  local copies, waits for them, and re-layouts: 0 us -> 15.6 us
    dot_general x1 -> x0, blocking collectives: 712 us -> none  [step(): jnp.einsum('rsntd,rsntf->rndf', a, g, preferred_element_type=jnp.float32)]
    pallas_call x0 -> x1, Pallas kernels: none -> 243 us  [sums(): pl.pallas_call(functools.partial(kernel, width), out_shape=jax.ShapeDtype...]
    dot_general x1 -> x0, matrix products: 167 us -> none  [step(): jnp.einsum('rsntd,rsntf->rndf', a, g, preferred_element_type=jnp.float32)]
    unnamed x0 -> x1, local copies, waits for them, and re-layouts: none -> 15.6 us
where the time goes in v1:
time: 259 us; the launch traced here: 258 us
  Pallas kernels  243 us (94%)
  local copies, waits for them, and re-layouts  15.6 us (6%)
    pallas_call x1, Pallas kernels, sums(): pl.pallas_call(functools.partial(kernel, width), out_shape=jax.ShapeDtype...  243 us
    unnamed x1, local copies, waits for them, and re-layouts  15.6 us

profile of v1, /device:TPU:0, one launch (start us, length us, event | category | flops | bytes accessed | tf_op | source)
XLA Modules:
  0.0 258.4 jit_solution(2858673056438844882)
XLA Ops:
  0.0 242.8 %grad_sums.1 = bf16[4,896,2560]{2,1,0:T(8,128)(2,1)} custom-call(bf16[4,8192,896]{2,1,0:T(8,128)(2,1)} %bitcast.2, bf16[4,8192,2560]{2,1,0:T(8,128)(2,1)} %bitcast.1.g_hbm), custom_call_target="tpu_custom_call" | custom-call | tf_op jit(solution)/shard_map/grad_sums/pallas_call | solution.py:216
  242.8 15.6 %copy.4 = bf16[4,896,2560]{2,1,0:T(8,128)(2,1)} copy(bf16[4,896,2560]{2,1,0:T(8,128)(2,1)} %grad_sums.1) | data formatting | bytes 36700160

commit v2 on v0

v2 whole, which is shorter than its diff:
```python
import functools

import jax
import jax.numpy as jnp
from jax import lax
from jax.experimental import pallas as pl
from jax.experimental.pallas import tpu as pltpu

COMBINE_LAG = {0: 1, 1: 5, 2: 3, 3: 1}
DELIVER_LAG = {0: 7, 1: 5, 2: 7, 3: 10}
PAIR_OUT, PAIR_IN, FROM_A, FROM_B, PART, RES = 2, 12, 12, 8, 6, 16
OWN = max(COMBINE_LAG.values()) + 1
SLICES = 4
BF16 = jnp.bfloat16


def groups(rows):
    first = (rows // 2 + 127) // 128 * 128
    return (0, first, first // 2), (first, rows - first, (rows - first) // 2)


def kernel(width, a_hbm, g_hbm, out, a_buf, g_buf, own, pair_out, pair_in, from_a, from_b, part,
           a_sem, g_sem, pair_ssem, pair_rsem, a_rsem, b_rsem, part_ssem, res_rsem, up_sem, down_sem,
           swap_ssem, swap_rsem):
    matrices, tokens, rows = a_hbm.shape
    per = g_hbm.shape[2] // width
    chunks = matrices * per
    blocks = 2 * chunks
    half = rows // 2
    depth = tokens // SLICES
    group = groups(rows)

    me = lax.axis_index("dp")
    chip, core = me // 2, me % 2
    place = chip + core * (3 - 2 * chip)
    step_to = 2 - 4 * core
    partner = me + 1 - 2 * core
    up, down = me + step_to, me - step_to

    barrier = pltpu.get_barrier_semaphore()

    def hello(device):
        pl.semaphore_signal(barrier, inc=1, device_id={"dp": device}, device_id_type=pl.DeviceIdType.MESH)

    hello(partner)
    pl.when(place > 0)(lambda: hello(down))
    pl.when(place < 3)(lambda: hello(up))

    def a_load(n, h, k):
        window = (pl.ds(k * depth, depth), pl.ds(group[h][0], group[h][1]))
        return pltpu.make_async_copy(a_hbm.at[(n, *window)], a_buf.at[(n % 2, *window)], a_sem.at[n % 2, h, k])

    def g_load(s):
        return pltpu.make_async_copy(
            g_hbm.at[s // per, :, pl.ds(pl.multiple_of((s % per) * width, width), width)], g_buf.at[s % 2],
            g_sem.at[s % 2])

    for h in range(2):
        for k in range(SLICES):
            a_load(0, h, k).start()
            if h == k == 0:
                g_load(0).start()
    pl.semaphore_wait(barrier, 1 + (place > 0).astype(jnp.int32) + (place < 3).astype(jnp.int32))

    def remote(src, dst, ssem, rsem, device):
        return pltpu.make_async_remote_copy(
            src_ref=src, dst_ref=dst, send_sem=ssem, recv_sem=rsem, device_id={"dp": device},
            device_id_type=pl.DeviceIdType.MESH)

    def pair_copy(b, h):
        r = pl.ds(0, group[h][2])
        return remote(pair_out.at[b % PAIR_OUT, r], pair_in.at[b % PAIR_IN, r], pair_ssem.at[b % PAIR_OUT],
                      pair_rsem.at[b % PAIR_IN], partner)

    def part_copy(b, h, box, rsem, slots, device):
        r = pl.ds(0, group[h][2])
        return remote(part.at[b % PART, r], box.at[b % slots, r], part_ssem.at[b % PART], rsem.at[b % slots], device)

    def to_a(b, h, device):
        return part_copy(b, h, from_a, a_rsem, FROM_A, device)

    def to_b(b, h, device):
        return part_copy(b, h, from_b, b_rsem, FROM_B, device)

    def spot(b, h):
        s = b // 2
        first, _, share = group[h]
        return out.at[s // per, pl.ds(pl.multiple_of(first + core * share, 16), share),
                      pl.ds(pl.multiple_of((s % per) * width, width), width)]

    def res_copy(b, h, ssem, device):
        return remote(spot(b, h), spot(b, h), ssem.at[b // 2 // per], res_rsem.at[b % RES], device)

    def swap_copy(b, h):
        n = b // 2 // per
        return remote(spot(b, h), spot(b, h), swap_ssem.at[n], swap_rsem.at[n], partner)

    def combine(d, b, h):
        pair_copy(b, h).wait_recv()
        r = pl.ds(0, group[h][2])
        if d == 2:
            to_a(b, h, up).wait_recv()
        if d == 1:
            to_a(b, h, down).wait_recv()
            to_b(b, h, up).wait_recv()
        total = own[b % OWN, r, :] + pair_in[b % PAIR_IN, r, :].astype(jnp.float32)
        if d in (1, 2):
            total += from_a[b % FROM_A, r, :].astype(jnp.float32)
        if d == 1:
            total += from_b[b % FROM_B, r, :].astype(jnp.float32)
            spot(b, h)[...] = total.astype(BF16)
            res_copy(b, h, up_sem, up).start()
            res_copy(b, h, down_sem, down).start()
            swap_copy(b, h).start()
            return
        copy = functools.partial(to_b if d == 2 else to_a, h=h, device=up if d == 0 else down)
        pl.when(b >= PART)(lambda: copy(b - PART).wait_send())
        part[b % PART, r, :] = total.astype(BF16)
        copy(b).start()

    def deliver(d, b, h):
        res_copy(b, h, up_sem, up).wait_recv()
        if d == 2:
            res_copy(b, h, up_sem, up).start()
        swap_copy(b, h).start()

    def each_place(f):
        for d in range(4):
            pl.when(place == d)(functools.partial(f, d))

    def guarded(b, f, *args):
        pl.when((b >= 0) & (b < blocks))(functools.partial(f, *args))

    def step(s, _):
        n, t = s // per, s % per
        for h in range(2):
            b = 2 * s + h

            @pl.when(s < chunks)
            def _():
                if h == 0:
                    pl.when(s + 1 < chunks)(lambda: g_load(s + 1).start())

                @pl.when((n + 1 < matrices) & (t < SLICES))
                def _():
                    a_load(n + 1, h, t).start()

                @pl.when(t == 0)
                def _():
                    for k in range(SLICES):
                        a_load(n, h, k).wait()

                if h == 0:
                    g_load(s).wait()
                first, count, share = group[h]
                r = pl.ds(0, share)
                term = lax.dot_general(
                    a_buf[n % 2, :, first:first + count], g_buf[s % 2], (((0,), (0,)), ((), ())),
                    preferred_element_type=jnp.float32)
                pl.when(b >= PAIR_OUT)(lambda: pair_copy(b - PAIR_OUT, h).wait_send())
                own[b % OWN, r, :] = jnp.where(core == 0, term[:share], term[share:])
                pair_out[b % PAIR_OUT, r, :] = jnp.where(core == 0, term[share:], term[:share]).astype(BF16)
                pair_copy(b, h).start()

            def stages(d):
                j = b - COMBINE_LAG[d]
                guarded(j, combine, d, j, (h - COMBINE_LAG[d]) % 2)
                if d != 1:
                    i = b - DELIVER_LAG[d]
                    guarded(i, deliver, d, i, (h - DELIVER_LAG[d]) % 2)

            each_place(stages)
        return 0

    lax.fori_loop(0, chunks + (max(DELIVER_LAG.values()) + 1) // 2, step, 0)

    for b in range(blocks - PAIR_OUT, blocks):
        pair_copy(b, b % 2).wait_send()

    def flush(d):
        if d != 1:
            for b in range(blocks - PART, blocks):
                to_a(b, b % 2, down).wait_send()
        for n in range(matrices):
            share = out.at[n, pl.ds(0, half), :]
            if d in (1, 2):
                remote(share, share, up_sem.at[n], swap_rsem.at[n], up).wait_send()
            if d == 1:
                remote(share, share, down_sem.at[n], swap_rsem.at[n], down).wait_send()
            swap = remote(share, share, swap_ssem.at[n], swap_rsem.at[n], partner)
            swap.wait_send()
            swap.wait_recv()

    each_place(flush)


def write(sums_ref, out_ref, sem):
    copies = [pltpu.make_async_copy(sums_ref.at[n], out_ref.at[n], sem.at[n]) for n in range(sums_ref.shape[0])]
    for c in copies:
        c.start()
    for c in copies:
        c.wait()


def sums(a, g, width=256):
    a, g = a[0], g[0]
    matrices, tokens, rows = a.shape
    shape = (matrices, rows, g.shape[2])
    share = groups(rows)[0][2]
    dma = pltpu.SemaphoreType.DMA
    anywhere, vmem = pl.BlockSpec(memory_space=pl.ANY), pl.BlockSpec(memory_space=pltpu.VMEM)
    held = pl.pallas_call(
        functools.partial(kernel, width),
        out_shape=pltpu.VMEM(shape, BF16),
        in_specs=[anywhere] * 2,
        out_specs=vmem,
        scratch_shapes=[
            pltpu.VMEM((2, tokens, rows), BF16),
            pltpu.VMEM((2, tokens, width), BF16),
            pltpu.VMEM((OWN, share, width), jnp.float32),
            pltpu.VMEM((PAIR_OUT, share, width), BF16),
            pltpu.VMEM((PAIR_IN, share, width), BF16),
            pltpu.VMEM((FROM_A, share, width), BF16),
            pltpu.VMEM((FROM_B, share, width), BF16),
            pltpu.VMEM((PART, share, width), BF16),
            dma((2, 2, SLICES)),
            dma((2,)),
            dma((PAIR_OUT,)),
            dma((PAIR_IN,)),
            dma((FROM_A,)),
            dma((FROM_B,)),
            dma((PART,)),
            dma((RES,)),
            dma((matrices,)),
            dma((matrices,)),
            dma((matrices,)),
            dma((matrices,)),
        ],
        compiler_params=pltpu.CompilerParams(collective_id=0, has_side_effects=True, vmem_limit_bytes=48_600_000),
        name="grad_sums",
    )(a, g)
    return pl.pallas_call(
        write,
        out_shape=jax.ShapeDtypeStruct(shape, BF16),
        in_specs=[vmem],
        out_specs=anywhere,
        scratch_shapes=[dma((matrices,))],
        compiler_params=pltpu.CompilerParams(vmem_limit_bytes=1 << 20),
        name="write_sums",
    )(held)


def solution(mesh):
    P = jax.sharding.PartitionSpec
    return jax.shard_map(
        sums, mesh=mesh, in_specs=(P(("rep", "dp")), P(("rep", "dp"))), out_specs=P("rep"), check_vma=False)
```

time: 879 us -> 234 us (0.27)
  blocking collectives: 712 us -> 0 us
  Pallas kernels: 0 us -> 234 us
  matrix products: 167 us -> 0 us
    dot_general x1 -> x0, blocking collectives: 712 us -> none  [step(): jnp.einsum('rsntd,rsntf->rndf', a, g, preferred_element_type=jnp.float32)]
    pallas_call x0 -> x2, Pallas kernels: none -> 234 us  [the longest x1 227 us: sums(): pl.pallas_call(functools.partial(kernel, width), out_shape=pltpu.VMEM(sha...]
    dot_general x1 -> x0, matrix products: 167 us -> none  [step(): jnp.einsum('rsntd,rsntf->rndf', a, g, preferred_element_type=jnp.float32)]
where the time goes in v2:
time: 234 us
  Pallas kernels  234 us (100%)
    pallas_call x1, Pallas kernels, sums(): pl.pallas_call(functools.partial(kernel, width), out_shape=pltpu.VMEM(sha...  227 us
    pallas_call x1, Pallas kernels, sums(): pl.pallas_call(write, out_shape=jax.ShapeDtypeStruct(shape, BF16), in_spe...  6.45 us

profile of v2, /device:TPU:0, one launch (start us, length us, event | category | flops | bytes accessed | tf_op | source)
XLA Modules:
  0.0 233.9 jit_solution(17352231916725844898)
XLA Ops:
  0.0 227.4 %grad_sums.1.sums_ref = bf16[4,896,2560]{2,1,0:T(8,128)(2,1)S(1)} custom-call(bf16[4,8192,896]{2,1,0:T(8,128)(2,1)} %bitcast.2, bf16[4,8192,2560]{2,1,0:T(8,128)(2,1)} %bitcast.1.g_hbm), custom_call_target="tpu_custom_call" | custom-call | tf_op jit(solution)/shard_map/grad_sums/pallas_call | solution.py:212
  227.4 6.4 %write_sums.1 = bf16[4,896,2560]{2,1,0:T(8,128)(2,1)} custom-call(bf16[4,896,2560]{2,1,0:T(8,128)(2,1)S(1)} %grad_sums.1.sums_ref), custom_call_target="tpu_custom_call" | custom-call | tf_op jit(solution)/shard_map/write_sums/pallas_call | solution.py:242

commit v3 on v2

v3 whole, which is shorter than its diff:
```python
import functools

import jax
import jax.numpy as jnp
from jax import lax
from jax.experimental import pallas as pl
from jax.experimental.pallas import tpu as pltpu

COMBINE_LAG = {1: 5, 2: 3, 3: 1}
DELIVER_LAG = {0: 10, 1: 8, 2: 6}
PAIR_OUT, PAIR_IN, FROM_A, FROM_B, PART, RES = 4, 24, 12, 12, 8, 16
OWN = 6
SLICES = 4
BF16 = jnp.bfloat16


def groups(rows):
    first = (rows // 2 + 127) // 128 * 128
    return (0, first, first // 2), (first, rows - first, (rows - first) // 2)


def kernel(width, a_hbm, g_hbm, out, a_buf, g_buf, own, pair_out, pair_in, from_a, from_b, part, held,
           a_sem, g_sem, pair_ssem, pair_rsem, a_rsem, b_rsem, part_ssem, res_rsem, down_sem, swap_ssem, swap_rsem):
    matrices, tokens, rows = a_hbm.shape
    per = g_hbm.shape[2] // width
    chunks = matrices * per
    blocks = 2 * chunks
    half = rows // 2
    depth = tokens // SLICES
    group = groups(rows)

    me = lax.axis_index("dp")
    chip, core = me // 2, me % 2
    place = 3 - chip + core * (2 * chip - 3)
    partner = me + 1 - 2 * core
    down, up = me + 2 - 4 * core, me - 2 + 4 * core
    beside = down + 1 - 2 * core

    barrier = pltpu.get_barrier_semaphore()

    def hello(device):
        pl.semaphore_signal(barrier, inc=1, device_id={"dp": device}, device_id_type=pl.DeviceIdType.MESH)

    hello(partner)
    pl.when(place > 0)(lambda: hello(down))
    pl.when(place < 3)(lambda: hello(up))
    pl.when(place == 3)(lambda: hello(beside))
    pl.when(place == 1)(lambda: hello(down + 1 - 2 * core))

    def a_load(n, h, k):
        window = (pl.ds(k * depth, depth), pl.ds(group[h][0], group[h][1]))
        return pltpu.make_async_copy(a_hbm.at[(n, *window)], a_buf.at[(n % 2, *window)], a_sem.at[n % 2, h, k])

    def g_load(s):
        return pltpu.make_async_copy(
            g_hbm.at[s // per, :, pl.ds(pl.multiple_of((s % per) * width, width), width)], g_buf.at[s % 2],
            g_sem.at[s % 2])

    g_load(0).start()
    for k in range(SLICES):
        a_load(0, 0, k).start()
    pl.semaphore_wait(barrier, jnp.where((place == 1) | (place == 3), 3 + (place == 1).astype(jnp.int32),
                                         2 + (place == 2).astype(jnp.int32)))

    def remote(src, dst, ssem, rsem, device):
        return pltpu.make_async_remote_copy(
            src_ref=src, dst_ref=dst, send_sem=ssem, recv_sem=rsem, device_id={"dp": device},
            device_id_type=pl.DeviceIdType.MESH)

    def pair_copy(i, h):
        r = pl.ds(0, group[h][2])
        return remote(pair_out.at[i % PAIR_OUT, r], pair_in.at[i % PAIR_IN, r], pair_ssem.at[i % PAIR_OUT],
                      pair_rsem.at[i % PAIR_IN], partner)

    def to_a(i, b, h, device):
        r = pl.ds(0, group[h][2])
        return remote(part.at[i % PART, r], from_a.at[b % FROM_A, r], part_ssem.at[i % PART], a_rsem.at[b % FROM_A],
                      device)

    def to_b(b, h):
        r = pl.ds(0, group[h][2])
        return remote(part.at[b % PART, r], from_b.at[b % FROM_B, r], part_ssem.at[b % PART], b_rsem.at[b % FROM_B],
                      down)

    def spot(b, h, c):
        s = b // 2
        first, _, share = group[h]
        whose = core if c == 0 else 1 - core
        return out.at[s // per, pl.ds(pl.multiple_of(first + whose * share, 16), share),
                      pl.ds(pl.multiple_of((s % per) * width, width), width)]

    def down_copy(b, h, c):
        return remote(spot(b, h, c), spot(b, h, c), down_sem.at[b // 2 // per, c], res_rsem.at[c, b % RES], down)

    def swap_copy(b, h, c, onward=False):
        n = b // 2 // per
        return remote(spot(b, h, c), spot(b, h, c), swap_ssem.at[n, c],
                      res_rsem.at[1, b % RES] if onward else swap_rsem.at[n, c], partner)

    def multiplied(d, b, h):
        share = group[h][2]
        r = pl.ds(0, share)
        mine = held[pl.ds(pl.multiple_of(core * share, 16), share), :]
        other = held[pl.ds(pl.multiple_of((1 - core) * share, 16), share), :]
        if d == 3:
            own[(2 * b) % OWN, r, :] = mine
            own[(2 * b + 1) % OWN, r, :] = other
            return
        if d == 0:
            for c, value in enumerate((other, mine)):
                i = 2 * b + c
                pl.when(i >= PAIR_OUT)(lambda: pair_copy(i - PAIR_OUT, (h - PAIR_OUT // 2) % 2).wait_send())
                pair_out[i % PAIR_OUT, r, :] = value.astype(BF16)
            for c in range(2):
                pair_copy(2 * b + c, h).start()
            return
        own[b % OWN, r, :] = mine
        pl.when(b >= PAIR_OUT)(lambda: pair_copy(b - PAIR_OUT, h).wait_send())
        pair_out[b % PAIR_OUT, r, :] = other.astype(BF16)
        pair_copy(b, h).start()

    def combine(d, b, h):
        r = pl.ds(0, group[h][2])

        def local(i):
            return own[i % OWN, r, :] + pair_in[i % PAIR_IN, r, :].astype(jnp.float32)

        if d == 3:
            for c, device in enumerate((down, beside)):
                i = 2 * b + c
                pair_copy(i, h).wait_recv()
                total = local(i)
                pl.when(i >= PART)(lambda: to_a(i - PART, b, (h - PART // 2) % 2, device).wait_send())
                part[i % PART, r, :] = total.astype(BF16)
                to_a(i, b, h, device).start()
            return
        pair_copy(b, h).wait_recv()
        to_a(b, b, h, up).wait_recv()
        if d == 1:
            to_b(b, h).wait_recv()
        total = local(b) + from_a[b % FROM_A, r, :].astype(jnp.float32)
        if d == 2:
            pl.when(b >= PART)(lambda: to_b(b - PART, h).wait_send())
            part[b % PART, r, :] = total.astype(BF16)
            to_b(b, h).start()
            return
        total += from_b[b % FROM_B, r, :].astype(jnp.float32)
        spot(b, h, 0)[...] = total.astype(BF16)
        down_copy(b, h, 0).start()
        swap_copy(b, h, 0, onward=True).start()

    def deliver(d, b, h):
        if d == 0:
            down_copy(b, h, 0).wait_recv()
            swap_copy(b, h, 0).start()
        down_copy(b, h, 1).wait_recv()
        if d != 0:
            down_copy(b, h, 1).start()
        if d != 2:
            swap_copy(b, h, 1).start()

    def each_place(f):
        for d in range(4):
            pl.when(place == d)(functools.partial(f, d))

    def guarded(b, f, *args):
        pl.when((b >= 0) & (b < blocks))(functools.partial(f, *args))

    def step(s, _):
        n, t = s // per, s % per
        for h in range(2):
            b = 2 * s + h

            @pl.when(s < chunks)
            def _():
                @pl.when(t == 0)
                def _():
                    for k in range(SLICES):
                        a_load(n, h, k).wait()

                if h == 0:
                    g_load(s).wait()

                    @pl.when(s == 0)
                    def _():
                        for k in range(SLICES):
                            a_load(0, 1, k).start()

                pl.when((s + 1 < chunks) & ((s == 0) if h else (s > 0)))(lambda: g_load(s + 1).start())

                @pl.when((n + 1 < matrices) & (t >= 1) & (t <= SLICES))
                def _():
                    a_load(n + 1, h, t - 1).start()

                first, count, _ = group[h]
                held[:count] = lax.dot_general(
                    a_buf[n % 2, :, first:first + count], g_buf[s % 2], (((0,), (0,)), ((), ())),
                    preferred_element_type=jnp.float32)
                each_place(lambda d: multiplied(d, b, h))

            def stages(d):
                if d != 0:
                    j = b - COMBINE_LAG[d]
                    guarded(j, combine, d, j, (h - COMBINE_LAG[d]) % 2)
                if d != 3:
                    i = b - DELIVER_LAG[d]
                    guarded(i, deliver, d, i, (h - DELIVER_LAG[d]) % 2)

            each_place(stages)
        return 0

    lax.fori_loop(0, chunks + (max(DELIVER_LAG.values()) + 1) // 2, step, 0)

    def flush(d):
        if d in (1, 2):
            for b in range(blocks - PAIR_OUT, blocks):
                pair_copy(b, b % 2).wait_send()
        if d == 0:
            for i in range(2 * blocks - PAIR_OUT, 2 * blocks):
                pair_copy(i, i // 2 % 2).wait_send()
        if d == 2:
            for b in range(blocks - PART, blocks):
                to_b(b, b % 2).wait_send()
        if d == 3:
            for i in range(2 * blocks - PART, 2 * blocks):
                to_a(i, i // 2, i // 2 % 2, down).wait_send()
        for n in range(matrices):
            share = out.at[n, pl.ds(0, half), :]
            for c in range(2):
                if d == 1 or (d == 2 and c == 1):
                    remote(share, share, down_sem.at[n, c], swap_rsem.at[n, c], down).wait_send()
                if d in (0, 1):
                    remote(share, share, swap_ssem.at[n, c], swap_rsem.at[n, c], partner).wait_send()
                if d == 3 or (d == 2 and c == 1):
                    remote(share, share, swap_ssem.at[n, c], swap_rsem.at[n, c], partner).wait_recv()

    each_place(flush)


def write(sums_ref, out_ref, sem):
    parts = sem.shape[1]
    rows = sums_ref.shape[1] // parts
    copies = [
        pltpu.make_async_copy(sums_ref.at[n, pl.ds(k * rows, rows), :], out_ref.at[n, pl.ds(k * rows, rows), :],
                              sem.at[n, k])
        for n in range(sums_ref.shape[0]) for k in range(parts)]
    for c in copies:
        c.start()
    for c in copies:
        c.wait()


def sums(a, g, width=256):
    a, g = a[0], g[0]
    matrices, tokens, rows = a.shape
    shape = (matrices, rows, g.shape[2])
    share = groups(rows)[0][2]
    dma = pltpu.SemaphoreType.DMA
    anywhere, vmem = pl.BlockSpec(memory_space=pl.ANY), pl.BlockSpec(memory_space=pltpu.VMEM)
    total = pl.pallas_call(
        functools.partial(kernel, width),
        out_shape=pltpu.VMEM(shape, BF16),
        in_specs=[anywhere] * 2,
        out_specs=vmem,
        scratch_shapes=[
            pltpu.VMEM((2, tokens, rows), BF16),
            pltpu.VMEM((2, tokens, width), BF16),
            pltpu.VMEM((OWN, share, width), jnp.float32),
            pltpu.VMEM((PAIR_OUT, share, width), BF16),
            pltpu.VMEM((PAIR_IN, share, width), BF16),
            pltpu.VMEM((FROM_A, share, width), BF16),
            pltpu.VMEM((FROM_B, share, width), BF16),
            pltpu.VMEM((PART, share, width), BF16),
            pltpu.VMEM((2 * share, width), jnp.float32),
            dma((2, 2, SLICES)),
            dma((2,)),
            dma((PAIR_OUT,)),
            dma((PAIR_IN,)),
            dma((FROM_A,)),
            dma((FROM_B,)),
            dma((PART,)),
            dma((2, RES)),
            dma((matrices, 2)),
            dma((matrices, 2)),
            dma((matrices, 2)),
        ],
        compiler_params=pltpu.CompilerParams(collective_id=0, has_side_effects=True, vmem_limit_bytes=48_600_000),
        name="grad_sums",
    )(a, g)
    return pl.pallas_call(
        write,
        out_shape=jax.ShapeDtypeStruct(shape, BF16),
        in_specs=[vmem],
        out_specs=anywhere,
        scratch_shapes=[dma((matrices, 4))],
        compiler_params=pltpu.CompilerParams(vmem_limit_bytes=1 << 20),
        name="write_sums",
    )(total)


def solution(mesh):
    P = jax.sharding.PartitionSpec
    return jax.shard_map(
        sums, mesh=mesh, in_specs=(P(("rep", "dp")), P(("rep", "dp"))), out_specs=P("rep"), check_vma=False)
```

time: 234 us -> 231 us (0.987)
  Pallas kernels: 234 us -> 231 us
    pallas_call x1, Pallas kernels: 227 us -> 225 us  [sums(): pl.pallas_call(functools.partial(kernel, width), out_shape=pltpu.VMEM(sha...]
where the time goes in v3:
time: 231 us
  Pallas kernels  231 us (100%)
    pallas_call x1, Pallas kernels, sums(): pl.pallas_call(functools.partial(kernel, width), out_shape=pltpu.VMEM(sha...  225 us
    pallas_call x1, Pallas kernels, sums(): pl.pallas_call(write, out_shape=jax.ShapeDtypeStruct(shape, BF16), in_spe...  6.45 us

profile of v3, /device:TPU:0, one launch (start us, length us, event | category | flops | bytes accessed | tf_op | source)
XLA Modules:
  0.0 231.3 jit_solution(3965691694749523010)
XLA Ops:
  0.0 224.9 %grad_sums.1.sums_ref = bf16[4,896,2560]{2,1,0:T(8,128)(2,1)S(1)} custom-call(bf16[4,8192,896]{2,1,0:T(8,128)(2,1)} %bitcast.2, bf16[4,8192,2560]{2,1,0:T(8,128)(2,1)} %bitcast.1.g_hbm), custom_call_target="tpu_custom_call" | custom-call | tf_op jit(solution)/shard_map/grad_sums/pallas_call | solution.py:260
  224.9 6.4 %write_sums.1 = bf16[4,896,2560]{2,1,0:T(8,128)(2,1)} custom-call(bf16[4,896,2560]{2,1,0:T(8,128)(2,1)S(1)} %grad_sums.1.sums_ref), custom_call_target="tpu_custom_call" | custom-call | tf_op jit(solution)/shard_map/write_sums/pallas_call | solution.py:290

commit v4 on v3

--- a/solution.py
+++ b/solution.py
@@ -6,8 +6,8 @@
 from jax.experimental import pallas as pl
 from jax.experimental.pallas import tpu as pltpu
 
-COMBINE_LAG = {1: 5, 2: 3, 3: 1}
-DELIVER_LAG = {0: 10, 1: 8, 2: 6}
+COMBINE_LAG = {1: 3, 2: 1, 3: 0}
+DELIVER_LAG = {0: 11, 1: 6, 2: 3}
 PAIR_OUT, PAIR_IN, FROM_A, FROM_B, PART, RES = 4, 24, 12, 12, 8, 16
 OWN = 6
 SLICES = 4
@@ -41,24 +41,28 @@
     def hello(device):
         pl.semaphore_signal(barrier, inc=1, device_id={"dp": device}, device_id_type=pl.DeviceIdType.MESH)
 
+    def a_load(n, h, k):
+        window = (pl.ds(k * depth, depth), pl.ds(group[h][0], group[h][1]))
+        return pltpu.make_async_copy(a_hbm.at[(n, *window)], a_buf.at[(n % 2, *window)], a_sem.at[n % 2, h, k])
+
+    def g_load(s):
+        return pltpu.make_async_copy(
+            g_hbm.at[s // per, :, pl.ds(pl.multiple_of((s % per) * width, width), width)], g_buf.at[s % 2],
+            g_sem.at[s % 2, 0])
+
+    def g_slice(k):
+        window = pl.ds(k * depth, depth)
+        return pltpu.make_async_copy(g_hbm.at[0, window, pl.ds(0, width)], g_buf.at[0, window], g_sem.at[0, k])
+
+    for k in range(SLICES):
+        g_slice(k).start()
+        a_load(0, 0, k).start()
+
     hello(partner)
     pl.when(place > 0)(lambda: hello(down))
     pl.when(place < 3)(lambda: hello(up))
     pl.when(place == 3)(lambda: hello(beside))
     pl.when(place == 1)(lambda: hello(down + 1 - 2 * core))
-
-    def a_load(n, h, k):
-        window = (pl.ds(k * depth, depth), pl.ds(group[h][0], group[h][1]))
-        return pltpu.make_async_copy(a_hbm.at[(n, *window)], a_buf.at[(n % 2, *window)], a_sem.at[n % 2, h, k])
-
-    def g_load(s):
-        return pltpu.make_async_copy(
-            g_hbm.at[s // per, :, pl.ds(pl.multiple_of((s % per) * width, width), width)], g_buf.at[s % 2],
-            g_sem.at[s % 2])
-
-    g_load(0).start()
-    for k in range(SLICES):
-        a_load(0, 0, k).start()
     pl.semaphore_wait(barrier, jnp.where((place == 1) | (place == 3), 3 + (place == 1).astype(jnp.int32),
                                          2 + (place == 2).astype(jnp.int32)))
 
@@ -173,29 +177,43 @@
 
             @pl.when(s < chunks)
             def _():
-                @pl.when(t == 0)
-                def _():
-                    for k in range(SLICES):
-                        a_load(n, h, k).wait()
-
-                if h == 0:
-                    g_load(s).wait()
-
-                    @pl.when(s == 0)
+                first, count, _ = group[h]
+
+                def multiply():
+                    @pl.when(t == 0)
                     def _():
                         for k in range(SLICES):
-                            a_load(0, 1, k).start()
-
-                pl.when((s + 1 < chunks) & ((s == 0) if h else (s > 0)))(lambda: g_load(s + 1).start())
-
-                @pl.when((n + 1 < matrices) & (t >= 1) & (t <= SLICES))
-                def _():
-                    a_load(n + 1, h, t - 1).start()
-
-                first, count, _ = group[h]
-                held[:count] = lax.dot_general(
-                    a_buf[n % 2, :, first:first + count], g_buf[s % 2], (((0,), (0,)), ((), ())),
-                    preferred_element_type=jnp.float32)
+                            a_load(n, h, k).wait()
+
+                    if h == 0:
+                        g_load(s).wait()
+                    pl.when((s + 1 < chunks) & ((s == 0) if h else (s > 0)))(lambda: g_load(s + 1).start())
+
+                    @pl.when((n + 1 < matrices) & (t >= 1) & (t <= SLICES))
+                    def _():
+                        a_load(n + 1, h, t - 1).start()
+
+                    held[:count] = lax.dot_general(
+                        a_buf[n % 2, :, first:first + count], g_buf[s % 2], (((0,), (0,)), ((), ())),
+                        preferred_element_type=jnp.float32)
+
+                def chase():
+                    for k in range(SLICES):
+                        a_load(0, 0, k).wait()
+                        g_slice(k).wait()
+                        for later in {1: (0,), 2: (1,), 3: (2, 3)}.get(k, ()):
+                            a_load(0, 1, later).start()
+                        window = slice(k * depth, (k + 1) * depth)
+                        term = lax.dot_general(
+                            a_buf[0, window, :count], g_buf[0, window], (((0,), (0,)), ((), ())),
+                            preferred_element_type=jnp.float32)
+                        held[:count] = term if k == 0 else held[:count] + term
+
+                if h == 0:
+                    pl.when(s == 0)(chase)
+                    pl.when(s > 0)(multiply)
+                else:
+                    multiply()
                 each_place(lambda d: multiplied(d, b, h))
 
             def stages(d):
@@ -273,7 +291,7 @@
             pltpu.VMEM((PART, share, width), BF16),
             pltpu.VMEM((2 * share, width), jnp.float32),
             dma((2, 2, SLICES)),
-            dma((2,)),
+            dma((2, SLICES)),
             dma((PAIR_OUT,)),
             dma((PAIR_IN,)),
             dma((FROM_A,)),

time: 231 us -> 229 us (level)
    pallas_call x1, Pallas kernels: 225 us -> 222 us  [sums(): pl.pallas_call(functools.partial(kernel, width), out_shape=pltpu.VMEM(sha...]
where the time goes in v4:
time: 229 us
  Pallas kernels  229 us (100%)
    pallas_call x1, Pallas kernels, sums(): pl.pallas_call(functools.partial(kernel, width), out_shape=pltpu.VMEM(sha...  222 us
    pallas_call x1, Pallas kernels, sums(): pl.pallas_call(write, out_shape=jax.ShapeDtypeStruct(shape, BF16), in_spe...  6.45 us

profile of v4, /device:TPU:0, one launch (start us, length us, event | category | flops | bytes accessed | tf_op | source)
XLA Modules:
  0.0 228.9 jit_solution(3361564316483204042)
XLA Ops:
  0.0 222.4 %grad_sums.1.sums_ref = bf16[4,896,2560]{2,1,0:T(8,128)(2,1)S(1)} custom-call(bf16[4,8192,896]{2,1,0:T(8,128)(2,1)} %bitcast.2, bf16[4,8192,2560]{2,1,0:T(8,128)(2,1)} %bitcast.1.g_hbm), custom_call_target="tpu_custom_call" | custom-call | tf_op jit(solution)/shard_map/grad_sums/pallas_call | solution.py:278
  222.5 6.4 %write_sums.1 = bf16[4,896,2560]{2,1,0:T(8,128)(2,1)} custom-call(bf16[4,896,2560]{2,1,0:T(8,128)(2,1)S(1)} %grad_sums.1.sums_ref), custom_call_target="tpu_custom_call" | custom-call | tf_op jit(solution)/shard_map/write_sums/pallas_call | solution.py:308
